TPU v7x, 32 devices: a whole 2x2x4 slice. The times are simulated.
32 devices in a mesh: grp: 2 (over y), col: 4 (over z), row: 2 (over x), dir: 2 (over core).
Axes of the slice: x: 2, y: 2, z: 4, core: 2. Of those that a mesh axis runs over, the one named last changes fastest.
Arguments:
- slopes_in: bfloat16 [512, 8192], P(None, ('grp', 'col')), parts along dimension 1, may hold values from -6 to 6
- basis_left: bfloat16 [12, 16, 256, 256], P(('row', 'dir'), 'col'), may hold values from -0.09375 to 0.09375
- basis_right: bfloat16 [12, 16, 256, 256], P(('row', 'dir'), 'col'), may hold values from -0.375 to 0.375
- rank_blocks: int32 [12, 16], P(('row', 'dir'), 'col'), may hold values from 1 to 4
- tile_owner: int32 [16], replicated, may hold values from 0 to 15, each once
- footprint: int32 [4, 4, 4, 2048], P(('row', 'dir')), may hold values from 0 to 767
- trace_weight: float32 [4, 4, 4, 2048], P(('row', 'dir')), may hold values from 0 to 0.5
- fitting: bfloat16 [2048, 4096], P(None, 'col'), may hold values from -0.125 to 0.125
Outputs:
- commands: bfloat16 [4, 1024, 4096], P(('row', 'dir'), 'grp', 'col'), parts along dimension 1
There are 2 independent parts, one for each index of `grp`. A program takes and returns all parts, laid end to end along the dimension named above; an argument that names none is the same for every part. Nothing has to cross between parts.
Inputs may be any that keep to these rules, and one draw needn't show every extreme that they name: rank_blocks[i, k] is the number of leading blocks of 64 columns of tile (i, k) that are live. `tile_owner`: each slope block appears in exactly one tile slot. `footprint`: indices into one layer's points.
All inputs are finite; a program needn't handle non-finite values.
Results may differ from a plain program's by a relative error of at most 0.0064.
Values may be sent and summed in bfloat16 or wider, within the bound.
No kernel may reach another device: no remote copies, remote signals or barrier semaphores. Data moves between devices by JAX's collectives and lax.ppermute only.
A program may use at most 128 MiB of HBM per device.

v0:
```python
import jax
import jax.numpy as jnp
from jax import lax
from jax.sharding import PartitionSpec as P

RB = 64


def shards(
    slopes_in, basis_left, basis_right, rank_blocks, tile_owner, footprint, trace_weight, fitting
):
    frames = slopes_in.shape[0]
    tile_size = basis_left.shape[2]
    rows_here = basis_left.shape[0]
    slots_here = basis_left.shape[1]
    rank_cols = basis_left.shape[3]
    owners = lax.dynamic_slice_in_dim(tile_owner, lax.axis_index("col") * slots_here, slots_here, 0)
    share = frames // lax.axis_size(("row", "dir"))
    mine = lax.dynamic_slice_in_dim(slopes_in, lax.axis_index(("row", "dir")) * share, share, 0)
    partial_value = lax.all_gather(mine, "col", axis=1, tiled=True)
    picked = jnp.take(partial_value.reshape(share, -1, tile_size), owners, axis=1)
    chosen = lax.all_gather(picked, ("row", "dir"), axis=0, tiled=True)
    columns = jnp.arange(rank_cols, dtype=jnp.int32) // RB
    live = columns[None, None, None, :] < rank_blocks[:, :, None, None]
    frame_share = frames // lax.axis_size("col")
    coeffs = jnp.einsum("fkn,iknr->ikfr", chosen, basis_right, preferred_element_type=jnp.float32)
    coeffs = jnp.where(live, coeffs, 0.0).astype(jnp.bfloat16)
    summed = jnp.einsum("ikfr,iknr->fin", coeffs, basis_left, preferred_element_type=jnp.float32)
    layer_block = lax.psum_scatter(
        summed.reshape(lax.axis_size("col") * frame_share, rows_here * tile_size),
        "col",
        scatter_dimension=0,
        tiled=True,
    ).astype(jnp.bfloat16)
    layers = lax.all_gather(layer_block, ("row", "dir"), axis=1, tiled=True)
    layer_count = footprint.shape[1]
    pupil_count = footprint.shape[3]
    per_layer = layers.shape[1] // layer_count
    shifts = (jnp.arange(layer_count, dtype=jnp.int32) * per_layer)[:, None, None]
    flat = (footprint[0] + shifts).reshape(-1)
    values = (
        jnp.take(layers, flat, axis=1)
        .astype(jnp.float32)
        .reshape(frame_share, layer_count, 4, pupil_count)
    )
    pupil = jnp.sum(values * trace_weight[0][None], axis=(1, 2)).astype(jnp.bfloat16)
    commands = jnp.dot(
        lax.all_gather(pupil, "col", axis=0, tiled=True),
        fitting,
        preferred_element_type=jnp.float32,
    )
    return commands.astype(jnp.bfloat16)[None]


def solution(mesh):
    placed = (
        P(None, ("grp", "col")),
        P(("row", "dir"), "col", None, None),
        P(("row", "dir"), "col", None, None),
        P(("row", "dir"), "col"),
        P(),
        P(("row", "dir"), None, None, None),
        P(("row", "dir"), None, None, None),
        P(None, "col"),
    )
    return jax.shard_map(
        shards,
        mesh=mesh,
        in_specs=placed,
        out_specs=P(("row", "dir"), "grp", "col"),
        check_vma=False,
    )
```

profile of v0, /device:TPU:0, one launch (start us, length us, event | category | flops | bytes accessed | tf_op | source)
XLA Modules:
  0.0 293.8 jit_solution(6185712206535708235)
XLA Ops:
  6.6 1.1 constant_dynamic-slice_fusion
  7.7 0.8 copy.14
  8.5 0.0 all-gather.6.cloned.1.call-start
  8.6 0.7 compare_and_fusion.1
  9.3 30.3 %all-gather.4.cloned.1.call-done = bf16[128,4096]{0,1:T(8,128)(2,1)} async-done(((bf16[128,1024]{0,1:T(8,128)(2,1)}), bf16[128,4096]{0,1:T(8,128)(2,1)}) %all-gather.4.cloned.1.call-update) | async-done | bytes 1048592 | tf_op jit(solution)/shard_map/all_gather | solution.py:20
  39.6 1.5 copy.12
  41.1 0.6 gather_fusion
  41.7 0.8 select_bitcast_fusion
  42.5 0.0 reduce-scatter.2.cloned.1.call-start
  42.6 0.1 add.67
  42.7 0.2 add.75
  42.9 0.2 squeeze.6
  43.1 0.1 broadcast_compare_fusion
  43.1 15.6 %all-gather.6.cloned.1.call-done = bf16[512,4,256]{2,0,1:T(8,128)(2,1)} async-done(((bf16[128,4,256]{2,0,1:T(8,128)(2,1)}), bf16[512,4,256]{2,0,1:T(8,128)(2,1)}) %all-gather.6.cloned.1.call-update) | async-done | bytes 1048592 | tf_op jit(solution)/shard_map/all_gather | solution.py:22
  58.8 4.7 %fusion.1 = f32[3,512,256,1]{1,2,3,0:T(8,128)} fusion(bf16[3,4,256,256]{3,2,1,0:T(8,128)(2,1)S(1)} %copy-done, pred[3,4,256]{2,1,0:T(4,128)(4,1)S(1)} %broadcast_compare_fusion, bf16[3,4,256,256]{3,2,1,0:T(8,128)(2,1)} %param.10, bf16[512,4,256]{2,0,1:T(8,128)(2,1)} %all-gather.6.cloned.1.call-done), kind=kOutput, calls=%fused_computation.5 | convolution fusion | flops 1613758464 | bytes 5770240 | tf_op jit(solution)/shard_map/ikfr,iknr->fin/dot_general | solution.py:28
  63.5 0.2 compare_select_fusion
  63.7 0.2 compare_and_fusion
  63.9 35.2 %reduce-scatter.2.cloned.1.call-done = f32[128,768]{0,1:T(8,128)} async-done(((f32[512,768]{0,1:T(8,128)}), f32[128,768]{0,1:T(8,128)}) %reduce-scatter.2.cloned.1.call-update) | async-done | bytes 393232 | tf_op jit(solution)/shard_map/reduce_scatter | solution.py:29
  99.1 1.0 convert_element_type.17
  100.1 8.6 %all_gather.14 = bf16[128,3072]{0,1:T(8,128)(2,1)S(1)} all-gather(bf16[128,768]{0,1:T(8,128)(2,1)S(1)} %convert_element_type.17), channel_id=1, replica_groups=mesh['grp'=2,'col'=4,'row'=2,'dir'=2] {'row','dir'}, dimensions={1}, use_global_device_ids=true | all-gather | bytes 983040 | tf_op jit(solution)/shard_map/all_gather | solution.py:35
  108.6 114.3 %gather_fusion.1 = bf16[32768,128]{1,0:T(8,128)(2,1)} fusion(bf16[128,3072]{0,1:T(8,128)(2,1)S(1)} %all_gather.14, s32[32768]{0:T(1024)S(1)} %broadcast_clamp_fusion), kind=kCustom, calls=%fused_computation.1 | custom fusion | bytes 16908288 | tf_op jit(solution)/shard_map/jit(_take)/gather | solution.py:42
  222.9 13.4 %multiply_reduce_fusion = bf16[128,2048]{0,1:T(8,128)(2,1)} fusion(f32[4,4,2048]{2,1,0:T(4,128)S(1)} %bitcast.39, bf16[128,4,4,2048]{0,3,2,1:T(8,128)(2,1)} %bitcast.35, pred[4,4,2048]{2,1,0:T(4,128)(4,1)S(1)} %compare_and_fusion), kind=kLoop, calls=%fused_computation.2 | loop fusion | flops 16515072 | bytes 9076736 | tf_op jit(solution)/shard_map/reduce_sum | solution.py:46
  236.3 44.8 %all-gather.8.cloned.1.call-done = bf16[512,2048]{0,1:T(8,128)(2,1)} async-done(((bf16[128,2048]{0,1:T(8,128)(2,1)}), bf16[512,2048]{0,1:T(8,128)(2,1)}) %all-gather.8.cloned.1.call-update) | async-done | bytes 2097168 | tf_op jit(solution)/shard_map/all_gather | solution.py:48
  281.2 6.1 %fusion.7 = bf16[1,512,1024]{2,1,0:T(8,128)(2,1)} fusion(bf16[512,2048]{0,1:T(8,128)(2,1)} %all-gather.8.cloned.1.call-done, bf16[2048,1024]{1,0:T(8,128)(2,1)} %param.15), kind=kOutput, calls=%fused_computation.10 | convolution fusion | flops 2148007936 | bytes 7340032 | tf_op jit(solution)/shard_map/dot_general | solution.py:47
  (18 shorter events, 0.2 us)
Async XLA Ops:
  6.5 52.2 %copy-start = (bf16[3,4,256,256]{3,2,1,0:T(8,128)(2,1)S(1)}, bf16[3,4,256,256]{3,2,1,0:T(8,128)(2,1)}, u32[]{:S(2)}) copy-start(bf16[3,4,256,256]{3,2,1,0:T(8,128)(2,1)} %param.9) | copy-start | bytes 4718596
  6.5 36.3 %copy-start.1 = (s32[1,4,4,2048]{3,2,1,0:T(4,128)S(1)}, s32[1,4,4,2048]{3,2,1,0:T(4,128)}, u32[]{:S(2)}) copy-start(s32[1,4,4,2048]{3,2,1,0:T(4,128)} %param.13) | copy-start | bytes 393220
  6.5 36.5 %copy-start.3 = (s32[3,4]{1,0:T(4,128)S(1)}, s32[3,4]{1,0:T(4,128)}, u32[]{:S(2)}) copy-start(s32[3,4]{1,0:T(4,128)} %param.11) | copy-start | bytes 148
  6.5 33.1 %all-gather.4.cloned.1.call-start = ((), (), s32[]{:S(2)}) async-start(), calls=%async_computation.1 | async-start | bytes 1310720 | tf_op jit(solution)/shard_map/all_gather | solution.py:20
  8.5 50.2 %all-gather.6.cloned.1.call-start = ((), (), s32[]{:S(2)}) async-start(), calls=%async_computation.2 | async-start | bytes 1310720 | tf_op jit(solution)/shard_map/all_gather | solution.py:22
  42.5 56.5 %reduce-scatter.2.cloned.1.call-start = ((), (), s32[]{:S(2)}) async-start(), calls=%async_computation.3 | async-start | bytes 1966080 | tf_op jit(solution)/shard_map/reduce_scatter | solution.py:29
  63.5 217.7 %all-gather.8.cloned.1.call-start = ((), (), s32[]{:S(2)}) async-start(), calls=%async_computation.4 | async-start | bytes 2621440 | tf_op jit(solution)/shard_map/all_gather | solution.py:48
  108.6 114.3 %copy-start.2 = (f32[1,4,4,2048]{3,2,1,0:T(4,128)S(1)}, f32[1,4,4,2048]{3,2,1,0:T(4,128)}, u32[]{:S(2)}) copy-start(f32[1,4,4,2048]{3,2,1,0:T(4,128)} %param.14) | copy-start | bytes 393220
Sparse Core Ops, SparseCore 0:
  8.9 30.6 all-gather.3
  42.6 16.0 all-gather.5
  63.6 35.4 reduce-scatter.1
  236.5 44.6 all-gather.7
where the time goes:
time: 294 us
  waiting for transfers between devices  126 us (43%)
  local copies, waits for them, and re-layouts  119 us (40%)
  other arithmetic  16.4 us (6%)
  between operations  13.2 us (4%)
  matrix products  10.8 us (4%)
  blocking collectives  8.58 us (3%)
    gather x1, local copies, waits for them, and re-layouts, shards(): jnp.take(layers, flat, axis=1).astype(jnp.float32)  114 us
    all_gather x1, waiting for transfers between devices, shards(): lax.all_gather(pupil, 'col', axis=0, tiled=True)  44.8 us
    reduce_scatter x1, waiting for transfers between devices, shards(): lax.psum_scatter(summed.reshape(lax.axis_size('col') * frame_share, rows_...  35.2 us
    all_gather x1, waiting for transfers between devices, shards(): partial_value = lax.all_gather(mine, 'col', axis=1, tiled=True)  30.3 us
    all_gather x1, waiting for transfers between devices, shards(): chosen = lax.all_gather(picked, ('row', 'dir'), axis=0, tiled=True)  15.6 us
    reduce_sum x1, other arithmetic, shards(): jnp.sum(values * trace_weight[0][None], axis=(1, 2)).astype(jnp.bfloat16)  13.4 us
    all_gather x1, blocking collectives, shards(): layers = lax.all_gather(layer_block, ('row', 'dir'), axis=1, tiled=True)  8.58 us
    dot_general x1, matrix products, shards(): jnp.dot(lax.all_gather(pupil, 'col', axis=0, tiled=True), fitting, prefer...  6.14 us
  transfers between devices with their start and end apart: 4, of which 4 were waited for; matrix products, arithmetic and copies ran while one was open for 1% of the time, Pallas kernels for 0%

commit v1 on v0

--- a/solution.py
+++ b/solution.py
@@ -17,7 +17,12 @@
     owners = lax.dynamic_slice_in_dim(tile_owner, lax.axis_index("col") * slots_here, slots_here, 0)
     share = frames // lax.axis_size(("row", "dir"))
     mine = lax.dynamic_slice_in_dim(slopes_in, lax.axis_index(("row", "dir")) * share, share, 0)
-    partial_value = lax.all_gather(mine, "col", axis=1, tiled=True)
+    ring = [mine]
+    for hop in range(3):
+        ring.append(lax.ppermute(ring[-1], "col", [(dev, (dev + 1) % 4) for dev in range(4)]))
+    partial_value = jnp.roll(
+        jnp.concatenate(ring[::-1], axis=1), (lax.axis_index("col") + 1) * ring[0].shape[1], axis=1
+    )
     picked = jnp.take(partial_value.reshape(share, -1, tile_size), owners, axis=1)
     chosen = lax.all_gather(picked, ("row", "dir"), axis=0, tiled=True)
     columns = jnp.arange(rank_cols, dtype=jnp.int32) // RB

time: 294 us -> 291 us (0.990)
  waiting for transfers between devices: 126 us -> 119 us
  starting transfers between devices: 0.13 us -> 3.2 us
    all_gather x1 -> x0, waiting for transfers between devices: 30.3 us -> none  [shards(): partial_value = lax.all_gather(mine, 'col', axis=1, tiled=True)]
    ppermute x0 -> x3, waiting for transfers between devices: none -> 25.3 us  [shards(): lax.ppermute(ring[-1], 'col', [(dev, (dev + 1) % 4) for dev in range(4)])]
    ppermute x0 -> x3, starting transfers between devices: none -> 3.11 us  [shards(): lax.ppermute(ring[-1], 'col', [(dev, (dev + 1) % 4) for dev in range(4)])]
  transfers between devices with their start and end apart: 4 -> 6, of which waited for: 4 -> 6; matrix products, arithmetic and copies ran while one was open for 1% -> 1% of each run, Pallas kernels for 0% -> 0%
where the time goes in v1:
time: 291 us
  local copies, waits for them, and re-layouts  119 us (41%)
  waiting for transfers between devices  119 us (41%)
  other arithmetic  16.4 us (6%)
  between operations  13.3 us (5%)
  matrix products  10.8 us (4%)
  blocking collectives  8.58 us (3%)
  starting transfers between devices  3.2 us (1%)
    gather x1, local copies, waits for them, and re-layouts, shards(): jnp.take(layers, flat, axis=1).astype(jnp.float32)  114 us
    all_gather x1, waiting for transfers between devices, shards(): lax.all_gather(pupil, 'col', axis=0, tiled=True)  44.8 us
    reduce_scatter x1, waiting for transfers between devices, shards(): lax.psum_scatter(summed.reshape(lax.axis_size('col') * frame_share, rows_...  35.2 us
    ppermute x3, waiting for transfers between devices, shards(): lax.ppermute(ring[-1], 'col', [(dev, (dev + 1) % 4) for dev in range(4)])  25.3 us
    all_gather x1, waiting for transfers between devices, shards(): chosen = lax.all_gather(picked, ('row', 'dir'), axis=0, tiled=True)  14 us
    reduce_sum x1, other arithmetic, shards(): jnp.sum(values * trace_weight[0][None], axis=(1, 2)).astype(jnp.bfloat16)  13.4 us
    all_gather x1, blocking collectives, shards(): layers = lax.all_gather(layer_block, ('row', 'dir'), axis=1, tiled=True)  8.58 us
    dot_general x1, matrix products, shards(): jnp.dot(lax.all_gather(pupil, 'col', axis=0, tiled=True), fitting, prefer...  6.14 us
  transfers between devices with their start and end apart: 6, of which 6 were waited for; matrix products, arithmetic and copies ran while one was open for 1% of the time, Pallas kernels for 0%

profile of v1, /device:TPU:0, one launch (start us, length us, event | category | flops | bytes accessed | tf_op | source)
XLA Modules:
  0.0 290.9 jit_solution(10171082950441653292)
XLA Ops:
  6.5 1.1 constant_dynamic-slice_fusion.1
  7.6 0.2 copy.14
  7.8 3.1 %collective-permute-start = (bf16[128,1024]{0,1:T(8,128)(2,1)S(1)}, bf16[128,1024]{0,1:T(8,128)(2,1)S(1)}, u32[]{:S(2)}, u32[]{:S(2)}) collective-permute-start(bf16[128,1024]{0,1:T(8,128)(2,1)S(1)} %copy.14), channel_id=1, source_target_pairs={{0,4},{4,8},{8,12},{12,0},{1,5},{5,9},{9,13},{13,1},{2,6},{6,10},{... | collective-permute-start | bytes 786440 | tf_op jit(solution)/shard_map/ppermute | solution.py:22
  10.9 8.3 %collective-permute-done = bf16[128,1024]{0,1:T(8,128)(2,1)S(1)} collective-permute-done((bf16[128,1024]{0,1:T(8,128)(2,1)S(1)}, bf16[128,1024]{0,1:T(8,128)(2,1)S(1)}, u32[]{:S(2)}, u32[]{:S(2)}) %collective-permute-start) | collective-permute-done | bytes 262176 | tf_op jit(solution)/shard_map/ppermute | solution.py:22
  19.2 9.3 %collective-permute-done.1 = bf16[128,1024]{0,1:T(8,128)(2,1)S(1)} collective-permute-done((bf16[128,1024]{0,1:T(8,128)(2,1)S(1)}, bf16[128,1024]{0,1:T(8,128)(2,1)S(1)}, u32[]{:S(2)}, u32[]{:S(2)}) %collective-permute-start.1) | collective-permute-done | bytes 262176 | tf_op jit(solution)/shard_map/ppermute | solution.py:22
  28.5 0.7 compare_and_fusion.1
  29.3 7.7 %collective-permute-done.2 = bf16[128,1024]{0,1:T(8,128)(2,1)S(1)} collective-permute-done((bf16[128,1024]{0,1:T(8,128)(2,1)S(1)}, bf16[128,1024]{0,1:T(8,128)(2,1)S(1)}, u32[]{:S(2)}, u32[]{:S(2)}) %collective-permute-start.2) | collective-permute-done | bytes 262176 | tf_op jit(solution)/shard_map/ppermute | solution.py:22
  37.4 1.3 copy.12
  38.7 1.8 gather_fusion
  40.5 0.8 select_bitcast_fusion
  41.3 0.1 add.80
  41.4 0.2 add.91
  41.6 0.2 squeeze.6
  41.9 14.0 %all-gather.3.cloned.1.call-done = bf16[512,4,256]{2,0,1:T(8,128)(2,1)} async-done(((bf16[128,4,256]{2,0,1:T(8,128)(2,1)}), bf16[512,4,256]{2,0,1:T(8,128)(2,1)}) %all-gather.3.cloned.1.call-update) | async-done | bytes 1048592 | tf_op jit(solution)/shard_map/all_gather | solution.py:27
  55.9 4.7 %fusion.1 = f32[3,512,256,1]{1,2,3,0:T(8,128)} fusion(bf16[3,4,256,256]{3,2,1,0:T(8,128)(2,1)S(1)} %copy-done, pred[3,4,256]{2,1,0:T(4,128)(4,1)S(1)} %broadcast_compare_fusion, bf16[3,4,256,256]{3,2,1,0:T(8,128)(2,1)} %param.10, bf16[512,4,256]{2,0,1:T(8,128)(2,1)} %all-gather.3.cloned.1.call-done), kind=kOutput, calls=%fused_computation.5 | convolution fusion | flops 1613758464 | bytes 5770240 | tf_op jit(solution)/shard_map/ikfr,iknr->fin/dot_general | solution.py:33
  60.7 0.2 compare_select_fusion
  60.9 0.2 compare_and_fusion
  61.1 35.2 %reduce-scatter.2.cloned.1.call-done = f32[128,768]{0,1:T(8,128)} async-done(((f32[512,768]{0,1:T(8,128)}), f32[128,768]{0,1:T(8,128)}) %reduce-scatter.2.cloned.1.call-update) | async-done | bytes 393232 | tf_op jit(solution)/shard_map/reduce_scatter | solution.py:34
  96.2 1.0 convert_element_type.17
  97.2 8.6 %all_gather.10 = bf16[128,3072]{0,1:T(8,128)(2,1)S(1)} all-gather(bf16[128,768]{0,1:T(8,128)(2,1)S(1)} %convert_element_type.17), channel_id=1, replica_groups=mesh['grp'=2,'col'=4,'row'=2,'dir'=2] {'row','dir'}, dimensions={1}, use_global_device_ids=true | all-gather | bytes 983040 | tf_op jit(solution)/shard_map/all_gather | solution.py:40
  105.8 114.2 %gather_fusion.1 = bf16[32768,128]{1,0:T(8,128)(2,1)} fusion(bf16[128,3072]{0,1:T(8,128)(2,1)S(1)} %all_gather.10, s32[32768]{0:T(1024)S(1)} %broadcast_clamp_fusion), kind=kCustom, calls=%fused_computation.1 | custom fusion | bytes 16908288 | tf_op jit(solution)/shard_map/jit(_take)/gather | solution.py:47
  220.0 13.4 %multiply_reduce_fusion = bf16[128,2048]{0,1:T(8,128)(2,1)} fusion(f32[4,4,2048]{2,1,0:T(4,128)S(1)} %bitcast.39, bf16[128,4,4,2048]{0,3,2,1:T(8,128)(2,1)} %bitcast.35, pred[4,4,2048]{2,1,0:T(4,128)(4,1)S(1)} %compare_and_fusion), kind=kLoop, calls=%fused_computation.2 | loop fusion | flops 16515072 | bytes 9076736 | tf_op jit(solution)/shard_map/reduce_sum | solution.py:51
  233.4 44.8 %all-gather.5.cloned.1.call-done = bf16[512,2048]{0,1:T(8,128)(2,1)} async-done(((bf16[128,2048]{0,1:T(8,128)(2,1)}), bf16[512,2048]{0,1:T(8,128)(2,1)}) %all-gather.5.cloned.1.call-update) | async-done | bytes 2097168 | tf_op jit(solution)/shard_map/all_gather | solution.py:53
  278.2 6.1 %fusion.7 = bf16[1,512,1024]{2,1,0:T(8,128)(2,1)} fusion(bf16[512,2048]{0,1:T(8,128)(2,1)} %all-gather.5.cloned.1.call-done, bf16[2048,1024]{1,0:T(8,128)(2,1)} %param.15), kind=kOutput, calls=%fused_computation.10 | convolution fusion | flops 2148007936 | bytes 7340032 | tf_op jit(solution)/shard_map/dot_general | solution.py:52
  (30 shorter events, 0.6 us)
Async XLA Ops:
  6.5 49.4 %copy-start = (bf16[3,4,256,256]{3,2,1,0:T(8,128)(2,1)S(1)}, bf16[3,4,256,256]{3,2,1,0:T(8,128)(2,1)}, u32[]{:S(2)}) copy-start(bf16[3,4,256,256]{3,2,1,0:T(8,128)(2,1)} %param.9) | copy-start | bytes 4718596
  6.5 49.4 %all-gather.3.cloned.1.call-start = ((), (), s32[]{:S(2)}) async-start(), calls=%async_computation.1 | async-start | bytes 1310720 | tf_op jit(solution)/shard_map/all_gather | solution.py:27
  7.8 11.4 %collective-permute-start = (bf16[128,1024]{0,1:T(8,128)(2,1)S(1)}, bf16[128,1024]{0,1:T(8,128)(2,1)S(1)}, u32[]{:S(2)}, u32[]{:S(2)}) collective-permute-start(bf16[128,1024]{0,1:T(8,128)(2,1)S(1)} %copy.14), channel_id=1, source_target_pairs={{0,4},{4,8},{8,12},{12,0},{1,5},{5,9},{9,13},{13,1},{2,6},{6,10},{... | collective-permute-start | bytes 786440 | tf_op jit(solution)/shard_map/ppermute | solution.py:22
  19.2 9.3 %collective-permute-start.1 = (bf16[128,1024]{0,1:T(8,128)(2,1)S(1)}, bf16[128,1024]{0,1:T(8,128)(2,1)S(1)}, u32[]{:S(2)}, u32[]{:S(2)}) collective-permute-start(bf16[128,1024]{0,1:T(8,128)(2,1)S(1)} %collective-permute-done), channel_id=1, source_target_pairs={{0,4},{4,8},{8,12},{12,0},{1,5},{5,9},{9,13},{13,1},{2,6},{6,10},{... | collective-permute-start | bytes 786440 | tf_op jit(solution)/shard_map/ppermute | solution.py:22
  28.5 8.4 %collective-permute-start.2 = (bf16[128,1024]{0,1:T(8,128)(2,1)S(1)}, bf16[128,1024]{0,1:T(8,128)(2,1)S(1)}, u32[]{:S(2)}, u32[]{:S(2)}) collective-permute-start(bf16[128,1024]{0,1:T(8,128)(2,1)S(1)} %collective-permute-done.1), channel_id=1, source_target_pairs={{0,4},{4,8},{8,12},{12,0},{1,5},{5,9},{9,13},{13,1},{2,6},{6,10},{... | collective-permute-start | bytes 786440 | tf_op jit(solution)/shard_map/ppermute | solution.py:22
  37.3 4.3 %copy-start.1 = (s32[1,4,4,2048]{3,2,1,0:T(4,128)S(1)}, s32[1,4,4,2048]{3,2,1,0:T(4,128)}, u32[]{:S(2)}) copy-start(s32[1,4,4,2048]{3,2,1,0:T(4,128)} %param.13) | copy-start | bytes 393220
  37.4 4.5 %copy-start.3 = (s32[3,4]{1,0:T(4,128)S(1)}, s32[3,4]{1,0:T(4,128)}, u32[]{:S(2)}) copy-start(s32[3,4]{1,0:T(4,128)} %param.11) | copy-start | bytes 148
  41.3 54.9 %reduce-scatter.2.cloned.1.call-start = ((), (), s32[]{:S(2)}) async-start(), calls=%async_computation.2 | async-start | bytes 1966080 | tf_op jit(solution)/shard_map/reduce_scatter | solution.py:34
  60.6 217.6 %all-gather.5.cloned.1.call-start = ((), (), s32[]{:S(2)}) async-start(), calls=%async_computation.3 | async-start | bytes 2621440 | tf_op jit(solution)/shard_map/all_gather | solution.py:53
  105.8 114.2 %copy-start.2 = (f32[1,4,4,2048]{3,2,1,0:T(4,128)S(1)}, f32[1,4,4,2048]{3,2,1,0:T(4,128)}, u32[]{:S(2)}) copy-start(f32[1,4,4,2048]{3,2,1,0:T(4,128)} %param.14) | copy-start | bytes 393220
Sparse Core Ops, SparseCore 0:
  41.4 14.4 all-gather.2
  60.7 35.4 reduce-scatter.1
  233.5 44.6 all-gather.4
